TPU v7x, 32 devices: a 4x4x1 block of a 4x4x8 slice. The times are simulated.
32 devices in a mesh: dp: 1 (over z), tp: 4 (over y), cp: 8 (over x, core).
Axes of the slice: x: 4, y: 4, z: 1, core: 2. Of those that a mesh axis runs over, the one named last changes fastest.
The devices are a block of a 4x4x8 slice.
Arguments:
- hidden: bfloat16 [24, 768, 768], P('dp', 'cp')
- tokens: int32 [24, 768], P('dp', 'cp')
- emb_table: bfloat16 [50304, 768], P('tp')
- out_table: bfloat16 [50304, 768], P('tp')
- w_proj: bfloat16 [768, 1536], replicated
- gain_h: float32 [768], replicated
- gain_e: float32 [768], replicated
- gain_f: float32 [768], replicated
Outputs:
- output 1: float32 [1], P('dp')
- output 2: bfloat16 [24, 768, 768], P('dp', 'cp')
- output 3: float32 [768, 1536], P('dp')
- output 4: float32 [50304, 768], P(('dp', 'tp'))
- output 5: float32 [50304, 768], P(('dp', 'tp'))
- output 6: float32 [768], P('dp')
- output 7: float32 [768], P('dp')
- output 8: float32 [768], P('dp')
All inputs are finite; a program needn't handle non-finite values.
Results may differ from a plain program's by a relative error of at most 0.001.
Values sent between devices are 32-bit elements.
A program may use at most 768 MiB of HBM per device.

v0:
```python
import jax
import jax.numpy as jnp
from jax import lax
from jax.sharding import PartitionSpec as P

MTP_WEIGHT = 0.3
NORM_EPS = 1e-6


def rms_norm(values, gain):
    scale = lax.rsqrt(jnp.mean(values * values, axis=-1, keepdims=True) + NORM_EPS)
    return values * scale * gain


def solution(mesh):
    cp_size = mesh.shape["cp"]
    shift_pairs = [(src + 1, src) for src in range(cp_size - 1)]

    def local_step(hidden, tokens, emb_blk, out_blk, w_proj, gain_h, gain_e, gain_f):
        batch, piece_len, width = hidden.shape
        vocab_blk = emb_blk.shape[0]
        tp_rank = lax.axis_index("tp")
        cp_rank = lax.axis_index("cp")
        seq_len = piece_len * cp_size
        next_head = lax.ppermute(tokens[:, :2], "cp", shift_pairs)
        ext_ids = jnp.concatenate([tokens, next_head], axis=1)
        next_ids = ext_ids[:, 1:piece_len + 1]
        label_ids = ext_ids[:, 2:]
        positions = cp_rank * piece_len + jnp.arange(piece_len)
        pos_weight = (positions < seq_len - 2).astype(jnp.float32)
        local_next = next_ids - tp_rank * vocab_blk
        in_block = (local_next >= 0) & (local_next < vocab_blk)
        emb_rows = jnp.take(emb_blk, jnp.clip(local_next, 0, vocab_blk - 1), axis=0).astype(jnp.float32)
        emb_rows = jnp.where(in_block[..., None], emb_rows, 0.0)
        emb_full = lax.psum(emb_rows, "tp")
        norm_h, vjp_h = jax.vjp(rms_norm, hidden.astype(jnp.float32), gain_h)
        norm_e, vjp_e = jax.vjp(rms_norm, emb_full, gain_e)
        joined = jnp.concatenate([norm_h.astype(jnp.bfloat16), norm_e.astype(jnp.bfloat16)], axis=-1)
        mixed = jnp.einsum("bsk,nk->bsn", joined, w_proj, preferred_element_type=jnp.float32)
        normed, vjp_f = jax.vjp(rms_norm, mixed, gain_f)
        features = normed.astype(jnp.bfloat16)
        logits = jnp.einsum("bsd,vd->bsv", features, out_blk, preferred_element_type=jnp.float32)
        row_max = lax.pmax(jnp.max(logits, axis=-1), "tp")
        local_label = label_ids - tp_rank * vocab_blk
        is_label = jnp.arange(vocab_blk) == local_label[..., None]
        exp_part = jnp.sum(jnp.exp(logits - row_max[..., None]), axis=-1)
        label_part = jnp.sum(jnp.where(is_label, logits, 0.0), axis=-1)
        exp_sum, label_logit = lax.psum((exp_part, label_part), "tp")
        log_norm = row_max + jnp.log(exp_sum)
        loss_part = jnp.sum(pos_weight * (log_norm - label_logit))
        soft_prob = jnp.exp(logits - log_norm[..., None])
        grad_logits = (MTP_WEIGHT * pos_weight[:, None] * (soft_prob - is_label.astype(jnp.float32))).astype(jnp.bfloat16)
        d_out = jnp.einsum("bsv,bsd->vd", grad_logits, features, preferred_element_type=jnp.float32)
        d_feats = lax.psum(jnp.einsum("bsv,vd->bsd", grad_logits, out_blk, preferred_element_type=jnp.float32), "tp")
        d_mixed, d_gain_f = vjp_f(d_feats)
        d_mixed_b = d_mixed.astype(jnp.bfloat16)
        d_proj = jnp.einsum("bsn,bsk->nk", d_mixed_b, joined, preferred_element_type=jnp.float32)
        d_joined = jnp.einsum("bsn,nk->bsk", d_mixed_b, w_proj, preferred_element_type=jnp.float32)
        d_hid, d_gain_h = vjp_h(d_joined[..., :width])
        d_embrow, d_gain_e = vjp_e(d_joined[..., width:])
        seg_ids = jnp.where(in_block, local_next, vocab_blk).reshape(-1)
        d_emb = jax.ops.segment_sum(d_embrow.reshape(-1, width), seg_ids, num_segments=vocab_blk)
        cp_totals = lax.psum((d_out, d_emb, d_proj, d_gain_h, d_gain_e, d_gain_f, loss_part), "cp")
        d_out, d_emb, d_proj, d_gain_h, d_gain_e, d_gain_f, loss_sum = cp_totals
        loss = (MTP_WEIGHT * loss_sum / (batch * (seq_len - 2))).reshape(1)
        return loss, d_hid.astype(jnp.bfloat16), d_proj, d_emb, d_out, d_gain_h, d_gain_e, d_gain_f

    part_seq = P("dp", "cp", None)
    in_specs = (part_seq, P("dp", "cp"), P("tp", None), P("tp", None), P(None, None), P(None), P(None), P(None))
    out_specs = (P("dp"), part_seq, P("dp", None), P(("dp", "tp"), None), P(("dp", "tp"), None), P("dp"), P("dp"), P("dp"))
    return jax.shard_map(local_step, mesh=mesh, in_specs=in_specs, out_specs=out_specs, check_vma=False)
```

profile of v0, /device:TPU:97, one launch (start us, length us, event | category | flops | bytes accessed | tf_op | source)
XLA Modules:
  0.0 1500.1 jit_solution(9662096740132593424)
XLA Ops:
  7.3 4.1 collective-permute-start
  11.4 2.0 collective-permute-done
  13.4 0.9 broadcast_select_fusion
  14.3 0.1 reshape.109
  14.4 18.4 %gather_fusion = bf16[2304,768]{1,0:T(8,128)(2,1)} fusion(bf16[12576,768]{1,0:T(8,128)(2,1)} %param.10, s32[3072]{0:T(1024)S(1)} %pad_clamp_fusion), kind=kCustom, calls=%fused_computation | custom fusion | bytes 7087104 | tf_op jit(solution)/shard_map/jit(_take)/gather | solution.py:33
  32.7 5.0 convert_select_fusion
  37.8 0.1 all-reduce.9.cloned.1.call-start
  37.8 0.5 compare_select_fusion.1
  38.3 0.5 compare_convert_fusion
  38.9 2.8 fusion.12
  41.7 0.6 copy-done.13
  42.3 0.6 copy-done.9
  42.9 4.7 fusion.8
  47.6 0.7 reshape.117
  48.2 126.3 %all-reduce.7.cloned.1.call-done = f32[24,96,768]{2,1,0:T(8,128)} async-done(((f32[24,96,768]{2,1,0:T(8,128)}), f32[24,96,768]{2,1,0:T(8,128)}) %all-reduce.7.cloned.1.call-update) | async-done | bytes 7077904 | tf_op jit(solution)/shard_map/psum | solution.py:35
  174.6 3.7 multiply_reduce_fusion.5
  178.3 0.6 copy-done.15
  178.9 0.7 copy-done.1
  179.6 0.7 multiply_convert_fusion.2
  180.3 0.6 copy-done.5
  180.9 8.0 multiply_reduce_fusion.4
  188.9 0.6 copy-done.19
  189.6 62.6 %fusion.26 = (f32[24,96]{1,0:T(8,128)S(1)}, f32[24,96,12576]{2,1,0:T(8,128)}) fusion(bf16[12576,768]{1,0:T(8,128)(2,1)} %param.11, f32[24,96,768]{2,1,0:T(8,128)} %get-tuple-element.37, f32[768]{0:T(1024)S(1)} %copy-done.25, f32[24,96]{1,0:T(8,128)S(1)} %fusion.23), kind=kOutput, calls=%fused_computation.70 | convolution fusion | flops 44540039168 | bytes 142316544 | tf_op jit(solution)/shard_map/bsd,vd->bsv/dot_general | solution.py:42
  252.1 11.3 pmax.7
  263.5 43.0 %select_reduce_fusion = (f32[24,96]{1,0:T(8,128)S(1)}, f32[24,96]{1,0:T(8,128)S(1)}) fusion(f32[24,96,12576]{2,1,0:T(8,128)} %get-tuple-element.39, s32[24,96]{1,0:T(8,128)S(1)} %get-tuple-element.33, f32[24,96]{1,0:T(8,128)S(1)} %pmax.7), kind=kLoop, calls=%fused_computation.3 | loop fusion | flops 144870912 | bytes 115937280 | tf_op jit(solution)/shard_map/reduce_sum | solution.py:47
  306.5 11.7 all-reduce.2
  318.1 0.6 multiply_reduce_fusion.6
  318.8 56.8 %multiply_convert_fusion = bf16[24,96,12576]{2,1,0:T(8,128)(2,1)} fusion(f32[24,96,12576]{2,1,0:T(8,128)} %get-tuple-element.39, f32[24,96]{1,0:T(8,128)S(1)} %get-tuple-element.30, f32[96]{0:T(128)S(1)} %copy-done.27, s32[24,96]{1,0:T(8,128)S(1)} %get-tuple-element.33), kind=kLoop, calls=%fused_computation.2 | loop fusion | flops 173850624 | bytes 173869440 | tf_op jit(solution)/shard_map/convert_element_type | solution.py:52
  375.5 55.3 %fusion = f32[24,96,768]{2,1,0:T(8,128)} fusion(bf16[24,96,12576]{2,1,0:T(8,128)(2,1)} %multiply_convert_fusion, bf16[12576,768]{1,0:T(8,128)(2,1)} %param.11), kind=kOutput, calls=%fused_computation.7 | convolution fusion | flops 44505759744 | bytes 84344832 | tf_op jit(solution)/shard_map/bsv,vd->bsd/dot_general | solution.py:54
  431.0 0.6 copy-done.18
  431.5 56.3 %convolution_bitcast_fusion = f32[12576,768]{1,0:T(8,128)} fusion(bf16[24,96,12576]{2,1,0:T(8,128)(2,1)} %multiply_convert_fusion, f32[24,96,768]{2,1,0:T(8,128)} %get-tuple-element.37, f32[768]{0:T(1024)S(1)} %copy-done.26, f32[24,96]{1,0:T(8,128)S(1)} %copy-done.18), kind=kOutput, calls=%fused_computation.6 | convolution fusion | flops 44511068160 | bytes 103673856 | tf_op jit(solution)/shard_map/bsv,bsd->vd/dot_general | solution.py:53
  487.9 84.4 %all-reduce.9.cloned.1.call-done = f32[24,96,768]{2,1,0:T(8,128)} async-done(((f32[24,96,768]{2,1,0:T(8,128)}), f32[24,96,768]{2,1,0:T(8,128)}) %all-reduce.9.cloned.1.call-update) | async-done | bytes 7077904 | tf_op jit(solution)/shard_map/psum | solution.py:54
  572.3 6.6 multiply_reduce_fusion
  578.9 0.4 copy-done.3
  579.4 2.0 copy-done.4
  581.4 1.5 fusion.10
  582.9 0.5 copy-done.6
  583.4 1.1 copy-done.8
  584.5 8.0 fusion.16
  592.6 5.7 fusion.17
  598.4 5.0 multiply_reduce_fusion.1
  603.4 5.4 add_add_fusion
  608.8 33.8 %scatter_custom_fusion = f32[12576,768]{1,0:T(8,128)} fusion(s32[2304]{0:T(1024)} %reshape.117, f32[2304,768]{1,0:T(8,128)} %bitcast.32, f32[]{:T(128)} %constant.21.clone.1), kind=kCustom, calls=%fused_computation.11 | custom fusion | flops 1769472 | bytes 38633984 | tf_op jit(solution)/shard_map/scatter-add | solution.py:62
  642.7 22.9 %all-reduce = (f32[]{:T(128)}, f32[768]{0:T(1024)}, f32[768]{0:T(1024)}, f32[768]{0:T(1024)}) all-reduce(f32[]{:T(128)} %get-tuple-element.29, f32[768]{0:T(1024)S(1)} %get-tuple-element.17, f32[768]{0:T(1024)S(1)} %get-tuple-element.10, f32[768]{0:T(1024)S(1)} %get-tuple-element.14), channel_id=1, replica_groups=mesh['dp'=1,'tp'=4,'cp'=8] {'cp'}, use_global_device_ids=true, to_apply=%region_11.12 | all-reduce | flops 2305 | bytes 18440 | tf_op jit(solution)/shard_map/psum | solution.py:63
  666.3 766.5 %all-reduce.11.cloned.1.call-done = (f32[768,1536]{1,0:T(8,128)}, f32[12576,768]{1,0:T(8,128)}, f32[12576,768]{1,0:T(8,128)}) async-done(((f32[768,1536]{1,0:T(8,128)}, f32[12576,768]{1,0:T(8,128)}, f32[12576,768]{1,0:T(8,128)}), (f32[768,1536]{1,0:T(8,128)}, f32[12576,768]{1,0:T(8,128)}, f32[12576,768]{1,0:T(8,128)})) %all-reduce.11.cloned.1.call-update) | async-done | bytes 81985552 | tf_op jit(solution)/shard_map/psum | solution.py:63
  1432.7 4.8 copy.21
  1437.6 27.3 %copy.22 = f32[12576,768]{1,0:T(8,128)} copy(f32[12576,768]{1,0:T(8,128)} %get-tuple-element.45) | data formatting | bytes 77266944
  1464.9 27.3 %copy.23 = f32[12576,768]{1,0:T(8,128)} copy(f32[12576,768]{1,0:T(8,128)} %get-tuple-element.46) | data formatting | bytes 77266944
  (65 shorter events, 0.5 us)
Async XLA Ops:
  7.2 173.1 %copy-start = (bf16[768,1536]{1,0:T(8,128)(2,1)S(1)}, bf16[768,1536]{1,0:T(8,128)(2,1)}, u32[]{:S(2)}) copy-start(bf16[768,1536]{1,0:T(8,128)(2,1)} %param.12) | copy-start | bytes 7077892
  7.2 167.4 %all-reduce.7.cloned.1.call-start = ((), (), s32[]{:S(2)}) async-start(), calls=%async_computation | async-start | bytes 14155776 | tf_op jit(solution)/shard_map/psum | solution.py:35
  7.3 6.1 collective-permute-start
  37.7 5.2 copy-start.21
  37.8 534.5 %all-reduce.9.cloned.1.call-start = ((), (), s32[]{:S(2)}) async-start(), calls=%async_computation.1 | async-start | bytes 14155776 | tf_op jit(solution)/shard_map/psum | solution.py:54
  41.7 0.6 copy-start.13
  42.3 0.6 copy-start.9
  42.9 136.0 %copy-start.23 = (f32[768]{0:T(1024)S(1)}, f32[768]{0:T(1024)}, u32[]{:S(2)}) copy-start(f32[768]{0:T(1024)} %param.14) | copy-start | bytes 9220
  174.6 5.0 copy-start.1
  178.3 0.6 copy-start.15
  178.9 2.0 copy-start.5
  179.6 9.3 copy-start.11
  180.9 8.0 copy-start.7
  180.9 8.6 copy-start.25
  188.9 0.6 copy-start.19
  189.5 62.6 %copy-start.17 = (f32[24,96]{1,0:T(8,128)}, f32[24,96]{1,0:T(8,128)S(1)}, u32[]{:S(2)}) copy-start(f32[24,96]{1,0:T(8,128)S(1)} %fusion.23) | copy-start | bytes 27652
  263.5 54.7 %copy-start.28 = (f32[96]{0:T(128)S(1)}, f32[96]{0:T(128)}, u32[]{:S(2)}) copy-start(f32[96]{0:T(128)} %compare_convert_fusion) | copy-start | bytes 1156
  263.5 55.3 %copy-start.27 = (f32[96]{0:T(128)S(1)}, f32[96]{0:T(128)}, u32[]{:S(2)}) copy-start(f32[96]{0:T(128)} %compare_select_fusion.1) | copy-start | bytes 1156
  430.8 0.7 copy-start.18
  430.8 0.7 copy-start.26
  430.9 1001.8 %all-reduce.11.cloned.1.call-start = ((), (), s32[]{:S(2)}) async-start(), calls=%async_computation.2 | async-start | bytes 163971072 | tf_op jit(solution)/shard_map/psum | solution.py:63
  487.9 91.0 %copy-start.20 = (f32[24,96]{1,0:T(8,128)S(1)}, f32[24,96]{1,0:T(8,128)}, u32[]{:S(2)}) copy-start(f32[24,96]{1,0:T(8,128)} %copy-done.19) | copy-start | bytes 27652
  572.3 7.1 copy-start.3
  572.3 9.1 copy-start.4
  581.4 2.0 copy-start.6
  581.4 3.1 copy-start.8
  584.5 13.8 slice-start
  592.5 5.8 slice-start.1
  592.5 5.8 copy-start.2
  592.5 5.8 copy-start.10
  592.6 5.8 copy-start.12
  592.6 5.8 copy-start.22
  592.6 5.8 copy-start.24
  598.3 5.0 copy-start.14
  598.4 5.0 copy-start.16
Sparse Core Ops, SparseCore 0:
  37.9 136.6 all-reduce.6
  431.0 141.2 all-reduce.8
  642.8 789.9 all-reduce.10
where the time goes:
time: 1510 us; the launch traced here: 1500 us
  waiting for transfers between devices  979 us (65%)
  matrix products  196 us (13%)
  other arithmetic  171 us (11%)
  local copies, waits for them, and re-layouts  86.9 us (6%)
  blocking collectives  45.9 us (3%)
  between operations  16.1 us (1%)
    psum x1, waiting for transfers between devices, local_step(): lax.psum((d_out, d_emb, d_proj, d_gain_h, d_gain_e, d_gain_f, loss_part),...  766 us
    psum x1, waiting for transfers between devices, local_step(): emb_full = lax.psum(emb_rows, 'tp')  126 us
    psum x1, waiting for transfers between devices, local_step(): lax.psum(jnp.einsum('bsv,vd->bsd', grad_logits, out_blk, preferred_elemen...  84.4 us
    unnamed x65, local copies, waits for them, and re-layouts  67.8 us
    dot_general x1, matrix products, local_step(): jnp.einsum('bsd,vd->bsv', features, out_blk, preferred_element_type=jnp.f...  62.6 us
    convert_element_type x1, other arithmetic, local_step(): (MTP_WEIGHT * pos_weight[:, None] * (soft_prob - is_label.astype(jnp.floa...  56.8 us
    dot_general x1, matrix products, local_step(): jnp.einsum('bsv,bsd->vd', grad_logits, features, preferred_element_type=j...  56.3 us
    dot_general x1, matrix products, local_step(): jnp.einsum('bsv,vd->bsd', grad_logits, out_blk, preferred_element_type=jn...  55.3 us
  transfers between devices with their start and end apart: 4, of which 4 were waited for; matrix products, arithmetic and copies ran while one was open for 4% of the time, Pallas kernels for 0%

commit v1 on v0

v1 whole, which is shorter than its diff:
```python
import functools

import jax
import jax.numpy as jnp
from jax import lax
from jax.experimental import pallas as pl
from jax.experimental.pallas import tpu as pltpu
from jax.sharding import PartitionSpec as P

MTP_WEIGHT = 0.3
NORM_EPS = 1e-6
CORES = 2
LANES = 128
SUBLANES = 8
GROUP = 8
MESH = pl.DeviceIdType.MESH


def rms_norm(values, gain):
    scale = lax.rsqrt(jnp.mean(values * values, axis=-1, keepdims=True) + NORM_EPS)
    return values * scale * gain


def gather_kernel(nx, ny, de_ref, dh_ref, de_all, dh_all, de_own, dh_own, own_sem, send_sem, pair_send, recv_sem, pair_recv, dh_send, dh_recv):
    y = lax.axis_index("tp")
    cp = lax.axis_index("cp")
    x = cp // CORES
    c = cp % CORES
    xr, xl = (x + 1) % nx, (x + nx - 1) % nx
    yr, yl = (y + 1) % ny, (y + ny - 1) % ny

    def at(xx, cc, yy):
        return {"tp": yy, "cp": xx * CORES + cc}

    peers = [at(xr, c, y), at(xl, c, y), at(x, c, yr), at(x, c, yl), at(x, 1 - c, y)]
    barrier = pltpu.get_barrier_semaphore()
    for peer in peers:
        pl.semaphore_signal(barrier, inc=1, device_id=peer, device_id_type=MESH)
    pl.semaphore_wait(barrier, len(peers))

    half = de_ref.shape[0] // 2
    dh_half = dh_ref.shape[0] // 2
    started = []

    def push(src, dst, ssem, rsem, peer):
        copy = pltpu.make_async_remote_copy(src_ref=src, dst_ref=dst, send_sem=ssem, recv_sem=rsem, device_id=peer, device_id_type=MESH)
        copy.start()
        started.append(copy)

    def slot(yy, xx, cc, part=None):
        ref = de_all.at[yy, xx, cc]
        return ref if part is None else ref.at[pl.ds(part * half, half)]

    n_sends = [0]

    def send(src, yy, xx, part, peer):
        k = n_sends[0]
        n_sends[0] += 1
        push(src, slot(yy, xx, c, part), send_sem.at[k], recv_sem.at[yy, xx, part or 0], peer)

    def to_pair(src, yy, xx):
        push(src, slot(yy, xx, c), pair_send.at[yy, xx], pair_recv.at[yy, xx], at(x, 1 - c, y))

    def arrived(yy, xx, part=None):
        ref = slot(yy, xx, c, part)
        pltpu.make_async_copy(ref, ref, recv_sem.at[yy, xx, part or 0]).wait()

    n_dh = [0]

    def send_dh(src, yy, part, peer):
        k = n_dh[0]
        n_dh[0] += 1
        dst = dh_all.at[yy]
        if part is not None:
            dst = dst.at[pl.ds(part * dh_half, dh_half)]
        push(src, dst, dh_send.at[k], dh_recv.at[yy, part or 0], peer)

    def dh_arrived(yy, part=None):
        ref = dh_all.at[yy]
        if part is not None:
            ref = ref.at[pl.ds(part * dh_half, dh_half)]
        pltpu.make_async_copy(ref, ref, dh_recv.at[yy, part or 0]).wait()

    send(de_ref, y, x, None, at(xr, c, y))
    send(de_ref, y, x, None, at(xl, c, y))
    send(de_ref, y, x, None, at(x, c, yr))
    send(de_ref, y, x, None, at(x, c, yl))
    to_pair(de_ref, y, x)
    send_dh(dh_ref, y, None, at(x, c, yr))
    send_dh(dh_ref, y, None, at(x, c, yl))
    own_in = [pltpu.make_async_copy(de_ref, de_own, own_sem.at[0]), pltpu.make_async_copy(dh_ref, dh_own, own_sem.at[1])]
    for copy in own_in:
        copy.start()
    for copy in own_in:
        copy.wait()
    own_out = [pltpu.make_async_copy(de_own, slot(y, x, c), own_sem.at[0]), pltpu.make_async_copy(dh_own, dh_all.at[y], own_sem.at[1])]
    for copy in own_out:
        copy.start()

    def row_block(xx):
        send(slot(y, xx, c), y, xx, None, at(x, c, yr))
        send(slot(y, xx, c), y, xx, None, at(x, c, yl))
        to_pair(slot(y, xx, c), y, xx)

    order = [x]
    for dist in range(1, nx // 2):
        left, right = (x + nx - dist) % nx, (x + dist) % nx
        last = dist + 1 == nx // 2
        arrived(y, left)
        part = 0 if last else None
        send(slot(y, left, c, part), y, left, part, at(xr, c, y))
        row_block(left)
        arrived(y, right)
        part = 1 if last else None
        send(slot(y, right, c, part), y, right, part, at(xl, c, y))
        row_block(right)
        order += [left, right]
    far = (x + nx // 2) % nx
    arrived(y, far, 0)
    arrived(y, far, 1)
    row_block(far)
    order.append(far)

    for dist in range(1, ny // 2):
        down, up = (y + ny - dist) % ny, (y + dist) % ny
        last = dist + 1 == ny // 2
        for k, xx in enumerate(order):
            arrived(down, xx)
            part = 0 if last else None
            send(slot(down, xx, c, part), down, xx, part, at(x, c, yr))
            to_pair(slot(down, xx, c), down, xx)
            arrived(up, xx)
            part = 1 if last else None
            send(slot(up, xx, c, part), up, xx, part, at(x, c, yl))
            to_pair(slot(up, xx, c), up, xx)
            if k == 0:
                for yy, part, peer in ((down, 0, yr), (up, 1, yl)):
                    part = part if last else None
                    dh_arrived(yy)
                    src = dh_all.at[yy] if part is None else dh_all.at[yy].at[pl.ds(part * dh_half, dh_half)]
                    send_dh(src, yy, part, at(x, c, peer))
    far_y = (y + ny // 2) % ny
    for xx in order:
        arrived(far_y, xx, 0)
        arrived(far_y, xx, 1)
        to_pair(slot(far_y, xx, c), far_y, xx)
    dh_arrived(far_y, 0)
    dh_arrived(far_y, 1)
    for yy in range(ny):
        for xx in range(nx):
            ref = slot(yy, xx, 1 - c)
            pltpu.make_async_copy(ref, ref, pair_recv.at[yy, xx]).wait()
    for copy in own_out:
        copy.wait()
    for copy in started:
        copy.wait_send()


def gather_rows(mesh, de_tiles, dh_rows):
    ny, nx = mesh.shape["tp"], mesh.shape["cp"] // CORES
    hbm = pl.BlockSpec(memory_space=pl.ANY)
    n_sends = 2 + 2 + 2 * (nx // 2 - 1) + 2 * (nx - 1) + 2 * nx * (ny // 2 - 1)
    n_dh = 2 + 2 * (ny // 2 - 1)
    dma = pltpu.SemaphoreType.DMA
    moved = 4 * ((nx * ny * CORES) * de_tiles.size + ny * dh_rows.size)
    return pl.pallas_call(
        functools.partial(gather_kernel, nx, ny),
        out_shape=(
            jax.ShapeDtypeStruct((ny, nx, CORES) + de_tiles.shape, jnp.float32),
            jax.ShapeDtypeStruct((ny,) + dh_rows.shape, jnp.float32),
        ),
        in_specs=[hbm, hbm],
        out_specs=(hbm, hbm),
        scratch_shapes=[
            pltpu.VMEM(de_tiles.shape, jnp.float32),
            pltpu.VMEM(dh_rows.shape, jnp.float32),
            dma((2,)),
            dma((n_sends,)),
            dma((ny, nx)),
            dma((ny, nx, 2)),
            dma((ny, nx)),
            dma((n_dh,)),
            dma((ny, 2)),
        ],
        compiler_params=pltpu.CompilerParams(collective_id=0, has_side_effects=True),
        cost_estimate=pl.CostEstimate(flops=400_000_000_000, bytes_accessed=moved, transcendentals=0),
        name="gather_rows",
    )(de_tiles, dh_rows)


def scatter_kernel(row_ref, dup_ref, de_ref, out_ref, acc, sem, *, chunk, lanes):
    step = pl.program_id(0)
    zero_rows = 4 * SUBLANES * lanes

    @pl.when(step == 0)
    def _():
        def zero(i, carry):
            acc[pl.ds(pl.multiple_of(i * zero_rows, SUBLANES), zero_rows), :] = jnp.zeros((zero_rows, LANES), jnp.float32)
            return carry

        lax.fori_loop(0, acc.shape[0] // zero_rows, zero, 0)

    def group(k, carry):
        first = step * chunk + k * GROUP
        source = k * (lanes * SUBLANES)
        shared = dup_ref[step * (chunk // GROUP) + k]

        @pl.when(shared == 0)
        def _():
            rows = [row_ref[first + m] for m in range(GROUP)]
            sums = [acc[pl.ds(rows[m], lanes, stride=SUBLANES), :] + de_ref[pl.ds(source + m, lanes, stride=SUBLANES), :] for m in range(GROUP)]
            for m in range(GROUP):
                acc[pl.ds(rows[m], lanes, stride=SUBLANES), :] = sums[m]

        @pl.when(shared != 0)
        def _():
            for m in range(GROUP):
                here = pl.ds(row_ref[first + m], lanes, stride=SUBLANES)
                acc[here, :] = acc[here, :] + de_ref[pl.ds(source + m, lanes, stride=SUBLANES), :]

        return carry

    lax.fori_loop(0, chunk // GROUP, group, 0)

    @pl.when(step == pl.num_programs(0) - 1)
    def _():
        copy = pltpu.make_async_copy(acc.at[pl.ds(0, out_ref.shape[0])], out_ref, sem.at[0])
        copy.start()
        copy.wait()


def scatter_rows(local_ids, valid, de_tiles, vocab_blk, width, chunk):
    lanes = width // LANES
    n = local_ids.shape[0]
    tiles = vocab_blk // SUBLANES
    place = jnp.arange(n, dtype=jnp.int32)
    spare = tiles * SUBLANES * lanes + place % SUBLANES
    rows = jnp.where(valid, (local_ids // SUBLANES) * (SUBLANES * lanes) + local_ids % SUBLANES, spare)
    grouped = rows.reshape(n // GROUP, GROUP)
    shared = jnp.zeros((n // GROUP,), jnp.bool_)
    for s in range(1, GROUP):
        shared = shared | jnp.any(grouped[:, s:] == grouped[:, : GROUP - s], axis=1)
    acc_tiles = -(-(tiles + 1) // 4) * 4
    out = pl.pallas_call(
        functools.partial(scatter_kernel, chunk=chunk, lanes=lanes),
        out_shape=jax.ShapeDtypeStruct((tiles * lanes * SUBLANES, LANES), jnp.float32),
        grid_spec=pltpu.PrefetchScalarGridSpec(
            num_scalar_prefetch=2,
            grid=(n // chunk,),
            in_specs=[pl.BlockSpec((chunk * lanes, LANES), lambda i, *_: (i, 0))],
            out_specs=pl.BlockSpec(memory_space=pl.ANY),
            scratch_shapes=[pltpu.VMEM((acc_tiles * SUBLANES * lanes, LANES), jnp.float32), pltpu.SemaphoreType.DMA((1,))],
        ),
        compiler_params=pltpu.CompilerParams(vmem_limit_bytes=60 * 1024 * 1024),
        cost_estimate=pl.CostEstimate(flops=100_000_000_000, bytes_accessed=4 * (n + vocab_blk) * width, transcendentals=0),
        name="scatter_rows",
    )(rows, shared.astype(jnp.int32), de_tiles)
    return out.reshape(tiles, lanes, SUBLANES, LANES).transpose(0, 2, 1, 3).reshape(vocab_blk, width)


def solution(mesh):
    cp_size = mesh.shape["cp"]
    tp_size = mesh.shape["tp"]
    shift_pairs = [(src + 1, src) for src in range(cp_size - 1)]

    def local_step(hidden, tokens, emb_blk, out_blk, w_proj, gain_h, gain_e, gain_f):
        batch, piece_len, width = hidden.shape
        vocab_blk = emb_blk.shape[0]
        lanes = width // LANES
        share = batch // tp_size
        tp_rank = lax.axis_index("tp")
        cp_rank = lax.axis_index("cp")
        seq_len = piece_len * cp_size
        next_head = lax.ppermute(tokens[:, :2], "cp", shift_pairs)
        ext_ids = jnp.concatenate([tokens, next_head], axis=1)
        next_ids = ext_ids[:, 1 : piece_len + 1]
        label_ids = ext_ids[:, 2:]
        positions = cp_rank * piece_len + jnp.arange(piece_len)
        pos_weight = (positions < seq_len - 2).astype(jnp.float32)
        local_next = next_ids - tp_rank * vocab_blk
        in_block = (local_next >= 0) & (local_next < vocab_blk)
        emb_rows = jnp.take(emb_blk, jnp.clip(local_next, 0, vocab_blk - 1), axis=0).astype(jnp.float32)
        emb_rows = jnp.where(in_block[..., None], emb_rows, 0.0)
        emb_full = lax.psum(emb_rows, "tp")
        all_next = lax.all_gather(next_ids, "cp")
        all_next = all_next.reshape(cp_size, tp_size, share * piece_len).transpose(1, 0, 2).reshape(-1)

        def front(hid, emb):
            joined = jnp.concatenate([rms_norm(hid, gain_h).astype(jnp.bfloat16), rms_norm(emb, gain_e).astype(jnp.bfloat16)], axis=-1)
            return joined, jnp.einsum("bsk,nk->bsn", joined, w_proj, preferred_element_type=jnp.float32)

        joined, mixed = front(hidden.astype(jnp.float32), emb_full)
        features = rms_norm(mixed, gain_f).astype(jnp.bfloat16)
        logits = jnp.einsum("bsd,vd->bsv", features, out_blk, preferred_element_type=jnp.float32)
        part_max = jnp.max(logits, axis=-1)
        local_label = label_ids - tp_rank * vocab_blk
        is_label = jnp.arange(vocab_blk) == local_label[..., None]
        part_sum = jnp.sum(jnp.exp(logits - part_max[..., None]), axis=-1)
        part_label = jnp.sum(jnp.where(is_label, logits, 0.0), axis=-1)
        stats = lax.all_gather(jnp.stack([part_max, part_sum, part_label]), "tp")
        row_max = jnp.max(stats[:, 0], axis=0)
        exp_sum = jnp.sum(stats[:, 1] * jnp.exp(stats[:, 0] - row_max), axis=0)
        label_logit = jnp.sum(stats[:, 2], axis=0)
        log_norm = row_max + jnp.log(exp_sum)
        loss_part = jnp.where(tp_rank == 0, jnp.sum(pos_weight * (log_norm - label_logit)), 0.0)
        soft_prob = jnp.exp(logits - log_norm[..., None])
        grad_logits = (MTP_WEIGHT * pos_weight[:, None] * (soft_prob - is_label.astype(jnp.float32))).astype(jnp.bfloat16)
        d_feats = jnp.einsum("bsv,vd->bsd", grad_logits, out_blk, preferred_element_type=jnp.float32)
        d_feats = lax.psum_scatter(d_feats, "tp", scatter_dimension=0, tiled=True)
        d_out = jnp.einsum("bsv,bsd->vd", grad_logits, features, preferred_element_type=jnp.float32)
        d_out = lax.psum(d_out, "cp")

        def mine(value):
            return lax.dynamic_slice_in_dim(value, tp_rank * share, share, axis=0)

        hid_f32 = mine(hidden).astype(jnp.float32)
        _, vjp_h = jax.vjp(rms_norm, hid_f32, gain_h)
        _, vjp_e = jax.vjp(rms_norm, mine(emb_full), gain_e)
        _, vjp_f = jax.vjp(rms_norm, mine(mixed), gain_f)
        d_mixed, d_gain_f = vjp_f(d_feats)
        d_mixed_b = d_mixed.astype(jnp.bfloat16)
        d_proj = jnp.einsum("bsn,bsk->nk", d_mixed_b, mine(joined), preferred_element_type=jnp.float32)
        d_joined = jnp.einsum("bsn,nk->bsk", d_mixed_b, w_proj, preferred_element_type=jnp.float32)
        d_hid, d_gain_h = vjp_h(d_joined[..., :width])
        d_embrow, d_gain_e = vjp_e(d_joined[..., width:])

        rows = share * piece_len
        de_tiles = d_embrow.reshape(rows // SUBLANES, SUBLANES, lanes, LANES).transpose(0, 2, 1, 3).reshape(rows * lanes, LANES)
        de_all, dh_all = gather_rows(mesh, de_tiles, d_hid.reshape(rows, width))
        local_all = all_next - tp_rank * vocab_blk
        owned = (local_all >= 0) & (local_all < vocab_blk)
        d_emb = scatter_rows(local_all, owned, de_all.reshape(-1, LANES), vocab_blk, width, rows)
        d_hidden = dh_all.reshape(batch, piece_len, width).astype(jnp.bfloat16)

        last = jnp.concatenate([d_gain_f, loss_part.reshape(1), jnp.zeros((width - 1,), jnp.float32)])
        packed = jnp.concatenate([d_proj, jnp.concatenate([d_gain_h, d_gain_e])[None], last[None], jnp.zeros((SUBLANES - 2, 2 * width), jnp.float32)])
        packed = lax.psum(packed, ("tp", "cp"))
        d_proj = packed[:width]
        d_gain_h, d_gain_e = packed[width, :width], packed[width, width:]
        d_gain_f, loss_sum = packed[width + 1, :width], packed[width + 1, width]
        loss = (MTP_WEIGHT * loss_sum / (batch * (seq_len - 2))).reshape(1)
        return loss, d_hidden, d_proj, d_emb, d_out, d_gain_h, d_gain_e, d_gain_f

    part_seq = P("dp", "cp", None)
    in_specs = (part_seq, P("dp", "cp"), P("tp", None), P("tp", None), P(None, None), P(None), P(None), P(None))
    out_specs = (P("dp"), part_seq, P("dp", None), P(("dp", "tp"), None), P(("dp", "tp"), None), P("dp"), P("dp"), P("dp"))
    return jax.shard_map(local_step, mesh=mesh, in_specs=in_specs, out_specs=out_specs, check_vma=False)
```

time: 1510 us -> 1060 us (0.70)
  waiting for transfers between devices: 979 us -> 190 us
  Pallas kernels: 0 us -> 408 us
  other arithmetic: 171 us -> 147 us
  local copies, waits for them, and re-layouts: 86.9 us -> 63.8 us
  blocking collectives: 45.9 us -> 30.5 us
    psum x2, waiting for transfers between devices: 851 us -> 26.1 us  [the longest x1 26.1 us: local_step(): d_out = lax.psum(d_out, 'cp')]
    pallas_call x0 -> x2, Pallas kernels: none -> 408 us  [the longest x1 305 us: gather_rows(): pl.pallas_call(functools.partial(gather_kernel, nx, ny), out_shape=(jax.S...]
    psum x2 -> x0, blocking collectives: 34.6 us -> none  [the longest x1 22.9 us: local_step(): lax.psum((d_out, d_emb, d_proj, d_gain_h, d_gain_e, d_gain_f, loss_part),...]
    scatter-add x1 -> x0, other arithmetic: 33.8 us -> none  [local_step(): jax.ops.segment_sum(d_embrow.reshape(-1, width), seg_ids, num_segments=vo...]
    unnamed x65 -> x53, local copies, waits for them, and re-layouts: 67.8 us -> 34.1 us
    reduce_scatter x0 -> x1, waiting for transfers between devices: none -> 31.4 us  [local_step(): d_feats = lax.psum_scatter(d_feats, 'tp', scatter_dimension=0, tiled=True)]
    all_gather x0 -> x2, blocking collectives: none -> 30.5 us  [the longest x1 21.3 us: local_step(): all_next = lax.all_gather(next_ids, 'cp')]
    reduce_sum x2 -> x4, other arithmetic: 43.6 us -> 37.1 us  [the longest x1 36.4 us: local_step(): part_sum = jnp.sum(jnp.exp(logits - part_max[..., None]), axis=-1)]
  transfers between devices with their start and end apart: 4 -> 5, of which waited for: 4 -> 4; matrix products, arithmetic and copies ran while one was open for 4% -> 9% of each run, Pallas kernels for 0% -> 39%
where the time goes in v1:
time: 1060 us; the launch traced here: 1050 us
  Pallas kernels  408 us (38%)
  waiting for transfers between devices  190 us (18%)
  matrix products  188 us (18%)
  other arithmetic  147 us (14%)
  local copies, waits for them, and re-layouts  63.8 us (6%)
  blocking collectives  30.5 us (3%)
  between operations  17.1 us (2%)
    pallas_call x1, Pallas kernels, gather_rows(): pl.pallas_call(functools.partial(gather_kernel, nx, ny), out_shape=(jax.S...  305 us
    psum x1, waiting for transfers between devices, local_step(): emb_full = lax.psum(emb_rows, 'tp')  130 us
    pallas_call x1, Pallas kernels, scatter_rows(): pl.pallas_call(functools.partial(scatter_kernel, chunk=chunk, lanes=lanes...  103 us
    dot_general x1, matrix products, local_step(): jnp.einsum('bsd,vd->bsv', features, out_blk, preferred_element_type=jnp.f...  62.6 us
    convert_element_type x1, other arithmetic, local_step(): (MTP_WEIGHT * pos_weight[:, None] * (soft_prob - is_label.astype(jnp.floa...  56.9 us
    dot_general x1, matrix products, local_step(): jnp.einsum('bsv,bsd->vd', grad_logits, features, preferred_element_type=j...  56 us
    dot_general x1, matrix products, local_step(): jnp.einsum('bsv,vd->bsd', grad_logits, out_blk, preferred_element_type=jn...  55.3 us
    reduce_sum x1, other arithmetic, local_step(): part_sum = jnp.sum(jnp.exp(logits - part_max[..., None]), axis=-1)  36.4 us
  transfers between devices with their start and end apart: 5, of which 4 were waited for; matrix products, arithmetic and copies ran while one was open for 9% of the time, Pallas kernels for 39%

profile of v1, /device:TPU:97, one launch (start us, length us, event | category | flops | bytes accessed | tf_op | source)
XLA Modules:
  0.0 1048.8 jit_solution(14935043403202200441)
XLA Ops:
  7.3 4.1 collective-permute-start
  11.4 2.0 collective-permute-done
  13.4 0.8 compare_and_fusion.1
  14.9 18.4 %gather_fusion = bf16[2304,768]{1,0:T(8,128)(2,1)} fusion(bf16[12576,768]{1,0:T(8,128)(2,1)} %param.10, s32[3072]{0:T(1024)S(1)} %pad_clamp_fusion), kind=kCustom, calls=%fused_computation | custom fusion | bytes 7087104 | tf_op jit(solution)/shard_map/jit(_take)/gather | solution.py:282
  33.2 5.0 convert_select_fusion
  39.4 2.8 fusion.5
  42.3 2.7 fusion.7
  45.0 130.1 %all-reduce.4.cloned.1.call-done = f32[24,96,768]{2,1,0:T(8,128)} async-done(((f32[24,96,768]{2,1,0:T(8,128)}), f32[24,96,768]{2,1,0:T(8,128)}) %all-reduce.4.cloned.1.call-update) | async-done | bytes 7077904 | tf_op jit(solution)/shard_map/psum | solution.py:284
  175.1 3.7 multiply_reduce_fusion.1
  178.8 1.3 copy-done.2
  180.8 1.3 copy-done.4
  182.1 8.3 multiply_reduce_fusion
  190.4 62.6 %fusion.55 = (f32[24,96]{1,0:T(8,128)S(1)}, f32[24,96,12576]{2,1,0:T(8,128)}) fusion(bf16[12576,768]{1,0:T(8,128)(2,1)} %param.11, f32[24,96,768]{2,1,0:T(8,128)} %get-tuple-element.34, f32[768]{0:T(1024)S(1)} %copy-done.20, f32[24,96]{1,0:T(8,128)S(1)} %add_rsqrt_fusion), kind=kOutput, calls=%fused_computation.143 | convolution fusion | flops 44540039168 | bytes 142316544 | tf_op jit(solution)/shard_map/bsd,vd->bsv/dot_general | solution.py:294
  253.1 36.4 %exponential_reduce_fusion = (f32[24,96]{1,0:T(8,128)S(1)}, f32[24,96]{1,0:T(8,128)S(1)}) fusion(f32[24,96,12576]{2,1,0:T(8,128)} %get-tuple-element.36, f32[24,96]{1,0:T(8,128)S(1)} %get-tuple-element.35, s32[24,96]{1,0:T(8,128)S(1)} %fusion.48), kind=kLoop, calls=%fused_computation.4 | loop fusion | flops 144870912 | bytes 115937280 | tf_op jit(solution)/shard_map/reduce_sum | solution.py:298
  289.5 9.2 all-gather
  299.4 56.9 %multiply_convert_fusion = bf16[24,96,12576]{2,1,0:T(8,128)(2,1)} fusion(f32[24,96,12576]{2,1,0:T(8,128)} %get-tuple-element.36, f32[24,96]{1,0:T(8,128)S(1)} %get-tuple-element.26, s32[24,96]{1,0:T(8,128)S(1)} %fusion.48, f32[96]{0:T(128)S(1)} %copy-done.24), kind=kLoop, calls=%fused_computation.1 | loop fusion | flops 173850624 | bytes 173869440 | tf_op jit(solution)/shard_map/convert_element_type | solution.py:307
  356.3 55.3 %fusion = f32[24,96,768]{2,1,0:T(8,128)} fusion(bf16[24,96,12576]{2,1,0:T(8,128)(2,1)} %multiply_convert_fusion, bf16[12576,768]{1,0:T(8,128)(2,1)} %param.11), kind=kOutput, calls=%fused_computation.6 | convolution fusion | flops 44505759744 | bytes 84344832 | tf_op jit(solution)/shard_map/bsv,vd->bsd/dot_general | solution.py:308
  411.9 1.4 fusion.12
  413.9 21.3 %all-gather.1 = s32[192,96]{1,0:T(8,128)S(1)} all-gather(s32[24,96]{1,0:T(8,128)S(1)} %copy-done.12), channel_id=3, replica_groups=mesh['dp'=1,'tp'=4,'cp'=8] {'cp'}, dimensions={0}, use_global_device_ids=true | all-gather | bytes 82944 | tf_op jit(solution)/shard_map/all_gather | solution.py:285
  435.9 1.3 sub.86
  437.2 1.6 sub.84
  438.8 1.8 fusion.20
  440.6 0.7 fusion.27
  441.3 0.7 fusion.28
  442.1 0.7 fusion.29
  442.8 0.7 fusion.30
  444.2 0.7 fusion.32
  446.3 0.7 fusion.36.row_ref
  447.7 1.7 multiply_reduce_fusion.7
  449.3 1.7 multiply_reduce_fusion.5
  451.1 31.4 %reduce-scatter.2.cloned.1.call-done = f32[6,96,768]{2,1,0:T(8,128)} async-done(((f32[24,96,768]{2,1,0:T(8,128)}), f32[6,96,768]{2,1,0:T(8,128)}) %reduce-scatter.2.cloned.1.call-update) | async-done | bytes 1769488 | tf_op jit(solution)/shard_map/reduce_scatter | solution.py:309
  482.4 2.6 multiply_reduce_fusion.6
  485.1 1.9 fusion.11
  487.0 1.5 fusion.8
  489.0 1.1 copy-done.7
  490.1 4.2 convolution_bitcast_fusion.1
  494.3 3.2 fusion.15
  497.7 4.9 maximum_maximum_fusion
  503.3 56.0 %convolution_bitcast_fusion = f32[12576,768]{1,0:T(8,128)} fusion(bf16[24,96,12576]{2,1,0:T(8,128)(2,1)} %multiply_convert_fusion, f32[24,96,768]{2,1,0:T(8,128)} %get-tuple-element.34, f32[768]{0:T(1024)S(1)} %copy-done.21, f32[24,96]{1,0:T(8,128)S(1)} %copy-done.23), kind=kOutput, calls=%fused_computation.5 | convolution fusion | flops 44511068160 | bytes 103673856 | tf_op jit(solution)/shard_map/bsv,bsd->vd/dot_general | solution.py:310
  559.9 5.3 add_add_fusion
  565.2 305.3 %gather_rows.1 = (f32[4,4,2,3456,128]{4,3,2,1,0:T(8,128)}, f32[4,576,768]{2,1,0:T(8,128)}) custom-call(f32[3456,128]{1,0:T(8,128)} %bitcast.67, f32[576,768]{1,0:T(8,128)} %bitcast.66), custom_call_target="tpu_custom_call" | custom-call | flops 399999991808 | bytes 63700992 | tf_op jit(solution)/shard_map/gather_rows/pallas_call | solution.py:166
  870.5 5.1 convert_element_type.55
  875.6 103.2 %scatter_rows.1 = f32[75456,128]{1,0:T(8,128)} custom-call(s32[18432]{0:T(1024)} %fusion.36.row_ref, s32[2304]{0:T(1024)} %or_convert_fusion.dup_ref, f32[110592,128]{1,0:T(8,128)} %bitcast.77), custom_call_target="tpu_custom_call" | custom-call | flops 99999997952 | bytes 95256576 | tf_op jit(solution)/shard_map/scatter_rows/pallas_call | solution.py:244
  978.9 1.2 slice.118
  980.8 4.8 slice.119
  985.6 1.4 slice_reduce_fusion.1
  987.1 26.1 %all-reduce.8.cloned.1.call-done = f32[12576,768]{1,0:T(8,128)} async-done(((f32[12576,768]{1,0:T(8,128)}), f32[12576,768]{1,0:T(8,128)}) %all-reduce.8.cloned.1.call-update) | async-done | bytes 38633488 | tf_op jit(solution)/shard_map/psum | solution.py:311
  1013.2 27.5 %copy.27 = f32[12576,768]{1,0:T(8,128)} copy(f32[12576,768]{1,0:T(8,128)} %all-reduce.8.cloned.1.call-done) | data formatting | bytes 77266944
  (91 shorter events, 9.0 us)
Async XLA Ops:
  7.2 173.6 %copy-start = (bf16[768,1536]{1,0:T(8,128)(2,1)S(1)}, bf16[768,1536]{1,0:T(8,128)(2,1)}, u32[]{:S(2)}) copy-start(bf16[768,1536]{1,0:T(8,128)(2,1)} %param.12) | copy-start | bytes 7077892
  7.2 167.9 %all-reduce.4.cloned.1.call-start = ((), (), s32[]{:S(2)}) async-start(), calls=%async_computation.1 | async-start | bytes 14155776 | tf_op jit(solution)/shard_map/psum | solution.py:284
  7.3 6.1 collective-permute-start
  14.2 0.6 copy-start.11
  38.3 4.0 copy-start.14
  38.3 444.1 %reduce-scatter.2.cloned.1.call-start = ((), (), s32[]{:S(2)}) async-start(), calls=%async_computation.2 | async-start | bytes 8847360 | tf_op jit(solution)/shard_map/reduce_scatter | solution.py:309
  38.4 3.9 copy-start.3
  42.3 2.7 copy-start.13
  45.0 133.8 %copy-start.16 = (f32[768]{0:T(1024)S(1)}, f32[768]{0:T(1024)}, u32[]{:S(2)}) copy-start(f32[768]{0:T(1024)} %param.14) | copy-start | bytes 9220
  175.1 5.0 copy-start.2
  180.1 2.0 copy-start.4
  182.1 8.3 copy-start.6
  182.1 8.3 copy-start.20
  190.4 62.6 %copy-start.22 = (f32[24,96]{1,0:T(8,128)}, f32[24,96]{1,0:T(8,128)S(1)}, u32[]{:S(2)}) copy-start(f32[24,96]{1,0:T(8,128)S(1)} %add_rsqrt_fusion) | copy-start | bytes 27652
  253.1 45.7 %copy-start.25 = (f32[96]{0:T(128)S(1)}, f32[96]{0:T(128)}, u32[]{:S(2)}) copy-start(f32[96]{0:T(128)} %compare_convert_fusion) | copy-start | bytes 1156
  253.1 46.3 %copy-start.24 = (f32[96]{0:T(128)S(1)}, f32[96]{0:T(128)}, u32[]{:S(2)}) copy-start(f32[96]{0:T(128)} %compare_select_fusion.1) | copy-start | bytes 1156
  411.6 2.2 copy-start.12
  411.7 567.2 %all-reduce.6.cloned.1.call-start = ((), (), s32[]{:S(2)}) async-start(), calls=%async_computation.3 | async-start | bytes 9535488 | tf_op jit(solution)/shard_map/psum | solution.py:337
  413.3 0.6 copy-start.18
  443.5 2.8 copy-start.10
  444.9 37.5 %copy-start.21 = (f32[768]{0:T(1024)S(1)}, f32[768]{0:T(1024)}, u32[]{:S(2)}) copy-start(f32[768]{0:T(1024)} %param.15) | copy-start | bytes 9220
  482.4 2.7 copy-start.9
  487.0 2.0 copy-start.5
  487.0 3.1 copy-start.7
  490.0 4.2 copy-start.8
  490.0 4.2 copy-start.15
  490.0 4.2 copy-start.17
  502.5 0.7 copy-start.23
  502.6 510.5 %all-reduce.8.cloned.1.call-start = ((), (), s32[]{:S(2)}) async-start(), calls=%async_computation.4 | async-start | bytes 77266944 | tf_op jit(solution)/shard_map/psum | solution.py:311
  559.2 0.7 copy-start.19
  1013.2 27.5 %copy-start.1 = (bf16[768,1536]{1,0:T(8,128)(2,1)S(1)}, bf16[768,1536]{1,0:T(8,128)(2,1)}, u32[]{:S(2)}) copy-start(bf16[768,1536]{1,0:T(8,128)(2,1)} %param.12) | copy-start | bytes 7077892
Sparse Core Ops, SparseCore 0:
  38.4 136.6 all-reduce.3
  411.8 70.5 reduce-scatter.1
  502.7 113.9 all-reduce.5
  619.7 393.3 all-reduce.7
